TPU v7x, 256 devices: a whole 4x4x8 slice. The times are simulated.
256 devices in a mesh: section: 8 (over x, core), row: 8 (over y, z_lo), col: 4 (over z_hi).
Axes of the slice: x: 4, y: 4, z: 8 (z_hi: 4, z_lo: 2; z = z_hi * 2 + z_lo), core: 2. Of those that a mesh axis runs over, the one named last changes fastest.
Arguments:
- tokens: bfloat16 [4096, 4096], P(('section', 'col'), 'row'), may hold values from -6 to 6
- grad_gate: bfloat16 [8, 8, 128, 14336], P('section', None, 'row', 'col'), may hold values from -0.5 to 0.5
- grad_up: bfloat16 [8, 8, 128, 14336], P('section', None, 'row', 'col'), may hold values from -0.5 to 0.5
- slot_token: int32 [8, 8, 128], P('section'), may hold values from 0 to 511, as said below
Outputs:
- gate_weight_grad: bfloat16 [8, 4096, 14336], P('section', 'row', 'col')
- up_weight_grad: bfloat16 [8, 4096, 14336], P('section', 'row', 'col')
Inputs may be any that keep to these rules, and one draw needn't show every extreme that they name: slot_token[g, e, c] is a token of group g; every token of a group fills exactly two of its group's 8 * 128 slots, and every slot is filled.
All inputs are finite; a program needn't handle non-finite values.
Results may differ from a plain program's by a relative error of at most 0.001.
Values may be sent and summed in bfloat16 or wider, within the bound.
A program may use at most 256 MiB of HBM per device.

v0:
```python
import jax
import jax.numpy as jnp
from jax import lax
from jax.sharding import PartitionSpec as P


def outer_sum(picked, grads):
    return jnp.einsum("gecd,gecf->edf", picked, grads, preferred_element_type=jnp.float32)


def body(tokens, grad_gate, grad_up, slot_token):
    group_tokens = lax.all_gather(tokens, "col", axis=0, tiled=True)
    routed = jnp.take(group_tokens, slot_token[0], axis=0)[None]
    moved_gate, moved_up, moved_rows = (
        lax.all_to_all(grad_gate, "section", split_axis=1, concat_axis=0, tiled=True),
        lax.all_to_all(grad_up, "section", split_axis=1, concat_axis=0, tiled=True),
        lax.all_to_all(routed, "section", split_axis=1, concat_axis=0, tiled=True),
    )
    gate_sum = outer_sum(moved_rows, lax.all_gather(moved_gate, "row", axis=2, tiled=True))
    up_sum = outer_sum(moved_rows, lax.all_gather(moved_up, "row", axis=2, tiled=True))
    return (gate_sum.astype(jnp.bfloat16), up_sum.astype(jnp.bfloat16))


def solution(mesh):
    return jax.shard_map(
        body,
        mesh=mesh,
        in_specs=(
            P(("section", "col"), "row"),
            P("section", None, "row", "col"),
            P("section", None, "row", "col"),
            P("section", None, None),
        ),
        out_specs=(P("section", "row", "col"), P("section", "row", "col")),
        check_vma=False,
    )
```

profile of v0, /device:TPU:1, one launch (start us, length us, event | category | flops | bytes accessed | tf_op | source)
XLA Modules:
  0.0 356.2 jit_solution(7237141620580496689)
XLA Ops:
  7.2 0.0 all-gather.7.cloned.1.call-start
  7.2 21.1 %all_to_all.33 = bf16[1,8,16,3584]{3,2,0,1:T(8,128)(2,1)} all-to-all(bf16[1,8,16,3584]{3,2,0,1:T(8,128)(2,1)} %bitcast.49), channel_id=1, replica_groups=mesh['section'=8,'row'=8,'col'=4] {'section'}, dimensions={1} | all-to-all | bytes 1835008 | tf_op jit(solution)/shard_map/all_to_all | solution.py:16
  28.3 0.0 copy-start
  28.3 0.0 all-gather.7.cloned.1.call-update
  28.4 0.0 all-gather.5.cloned.1.call-start
  28.4 18.8 %all_to_all.34 = bf16[1,8,16,3584]{3,2,0,1:T(8,128)(2,1)} all-to-all(bf16[1,8,16,3584]{3,2,0,1:T(8,128)(2,1)} %bitcast.50), channel_id=1, replica_groups=mesh['section'=8,'row'=8,'col'=4] {'section'}, dimensions={1} | all-to-all | bytes 1835008 | tf_op jit(solution)/shard_map/all_to_all | solution.py:15
  47.2 0.0 all-gather.5.cloned.1.call-update
  47.2 21.4 %all_gather.9 = bf16[512,512]{1,0:T(8,128)(2,1)S(1)} all-gather(bf16[128,512]{1,0:T(8,128)(2,1)} %param.4), channel_id=1, replica_groups=mesh['section'=8,'row'=8,'col'=4] {'col'}, dimensions={0}, use_global_device_ids=true | all-gather | bytes 655360 | tf_op jit(solution)/shard_map/all_gather | solution.py:12
  68.7 0.7 fusion.17
  69.3 4.0 %gather_fusion = bf16[1024,512]{1,0:T(8,128)(2,1)S(1)} fusion(bf16[512,512]{1,0:T(8,128)(2,1)S(1)} %all_gather.9, s32[1024]{0:T(1024)S(1)} %fusion.17), kind=kCustom, calls=%fused_computation | custom fusion | bytes 2101248 | tf_op jit(solution)/shard_map/jit(_take)/gather | solution.py:13
  73.3 0.0 copy-done
  73.3 0.2 broadcast_select_fusion
  73.5 0.7 copy.7
  74.2 19.8 %all_to_all.35 = bf16[1,8,128,512]{2,3,0,1:T(8,128)(2,1)S(1)} all-to-all(bf16[1,8,128,512]{2,3,0,1:T(8,128)(2,1)S(1)} %copy.7), channel_id=1, replica_groups=mesh['section'=8,'row'=8,'col'=4] {'section'}, dimensions={1} | all-to-all | bytes 2097152 | tf_op jit(solution)/shard_map/all_to_all | solution.py:17
  94.0 93.9 %all-gather.7.cloned.1.call-done = bf16[1,8,128,3584]{3,2,1,0:T(8,128)(2,1)} async-done(((bf16[1,8,16,3584]{3,2,1,0:T(8,128)(2,1)}), bf16[1,8,128,3584]{3,2,1,0:T(8,128)(2,1)}) %all-gather.7.cloned.1.call-update) | async-done | bytes 7340048 | tf_op jit(solution)/shard_map/all_gather | solution.py:20
  187.8 7.5 %fusion.11 = bf16[1,512,3584]{2,1,0:T(8,128)(2,1)} fusion(bf16[1,8,128,3584]{3,2,1,0:T(8,128)(2,1)} %all-gather.7.cloned.1.call-done, bf16[1,8,128,512]{2,3,0,1:T(8,128)(2,1)S(1)} %all_to_all.35), kind=kOutput, calls=%fused_computation.8 | convolution fusion | flops 3759931392 | bytes 12058624 | tf_op jit(solution)/shard_map/gecd,gecf->edf/dot_general | solution.py:8
  195.3 146.6 %all-gather.5.cloned.1.call-done = bf16[1,8,128,3584]{3,2,1,0:T(8,128)(2,1)} async-done(((bf16[1,8,16,3584]{3,2,1,0:T(8,128)(2,1)}), bf16[1,8,128,3584]{3,2,1,0:T(8,128)(2,1)}) %all-gather.5.cloned.1.call-update) | async-done | bytes 7340048 | tf_op jit(solution)/shard_map/all_gather | solution.py:19
  341.9 7.5 %fusion.8 = bf16[1,512,3584]{2,1,0:T(8,128)(2,1)} fusion(bf16[1,8,128,3584]{3,2,1,0:T(8,128)(2,1)} %all-gather.5.cloned.1.call-done, bf16[1,8,128,512]{2,3,0,1:T(8,128)(2,1)S(1)} %all_to_all.35), kind=kOutput, calls=%fused_computation.7 | convolution fusion | flops 3759931392 | bytes 12058624 | tf_op jit(solution)/shard_map/gecd,gecf->edf/dot_general | solution.py:8
  (1 shorter events, 0.0 us)
Async XLA Ops:
  7.2 180.7 %all-gather.7.cloned.1.call-start = ((), (), s32[]{:S(2)}) async-start(), calls=%async_computation.4 | async-start | bytes 8257536 | tf_op jit(solution)/shard_map/all_gather | solution.py:20
  28.3 45.0 %copy-start = (s32[1,8,128]{2,1,0:T(8,128)S(1)}, s32[1,8,128]{2,1,0:T(8,128)}, u32[]{:S(2)}) copy-start(s32[1,8,128]{2,1,0:T(8,128)} %param.7) | copy-start | bytes 12292
  28.4 313.5 %all-gather.5.cloned.1.call-start = ((), (), s32[]{:S(2)}) async-start(), calls=%async_computation.3 | async-start | bytes 8257536 | tf_op jit(solution)/shard_map/all_gather | solution.py:19
Sparse Core Ops, SparseCore 0:
  28.5 159.2 all-gather.6
  189.6 152.1 all-gather.4
where the time goes:
time: 356 us
  waiting for transfers between devices  240 us (67%)
  blocking collectives  81.1 us (23%)
  matrix products  14.9 us (4%)
  between operations  14.1 us (4%)
  local copies, waits for them, and re-layouts  4.62 us (1%)
    all_gather x1, waiting for transfers between devices, body(): lax.all_gather(moved_gate, 'row', axis=2, tiled=True)  147 us
    all_gather x1, waiting for transfers between devices, body(): lax.all_gather(moved_up, 'row', axis=2, tiled=True)  93.9 us
    all_gather x1, blocking collectives, body(): group_tokens = lax.all_gather(tokens, 'col', axis=0, tiled=True)  21.4 us
    all_to_all x1, blocking collectives, body(): lax.all_to_all(grad_up, 'section', split_axis=1, concat_axis=0, tiled=True)  21.1 us
    all_to_all x1, blocking collectives, body(): lax.all_to_all(routed, 'section', split_axis=1, concat_axis=0, tiled=True)  19.8 us
    all_to_all x1, blocking collectives, body(): lax.all_to_all(grad_gate, 'section', split_axis=1, concat_axis=0, tiled=T...  18.8 us
    dot_general x2, matrix products, outer_sum(): jnp.einsum('gecd,gecf->edf', picked, grads, preferred_element_type=jnp.fl...  14.9 us
  transfers between devices with their start and end apart: 2, of which 2 were waited for; matrix products, arithmetic and copies ran while one was open for 4% of the time, Pallas kernels for 0%

commit v1 on v0

v1 whole, which is shorter than its diff:
```python
import functools

import jax
import jax.numpy as jnp
from jax import lax
from jax.experimental import pallas as pl
from jax.experimental.pallas import tpu as pltpu
from jax.sharding import PartitionSpec as P

NC = 14
LEAD = 3


def y_first(c):
    m = lax.rem(c, 5)
    return (m == 0) | (m == 2)


def kernel(
    n_sec, n_col,
    tok_ref, gate_ref, up_ref, slot_ref, out_gate, out_up,
    grads, toks, picked, lhs,
    tok_send, tok_recv, pick_send, pick_recv, sec_send, sec_recv, row_send, row_recv,
):
    s, r, k = lax.axis_index("section"), lax.axis_index("row"), lax.axis_index("col")
    y, z = r // 2, lax.rem(r, 2)

    def row_at(yy, zz):
        return lax.rem(yy + 8, 4) * 2 + zz

    y_up, y_down, z_other = row_at(y + 1, z), row_at(y - 1, z), row_at(y, 1 - z)
    rows = gate_ref.shape[2]
    wide = grads.shape[3]
    half = NC // 2
    n_tok = tok_ref.shape[0]
    cap = slot_ref.shape[2]

    def block(c, who):
        return grads.at[c, :, pl.ds(pl.multiple_of(who * rows, rows), rows), :]

    def piece(c, group):
        return grads.at[c, group, pl.ds(pl.multiple_of(r * rows, rows), rows), :]

    def row_copy(c, who, to):
        return pltpu.make_async_remote_copy(
            src_ref=block(c, who), dst_ref=block(c, who),
            send_sem=row_send.at[c], recv_sem=row_recv.at[c, who], device_id={"row": to},
        )

    def arrived(c, who):
        row_copy(c, who, y_up).wait_recv()

    barrier = pltpu.get_barrier_semaphore()

    def greet(axis, me, n):
        def one(j, carry):
            pl.semaphore_signal(barrier, inc=1, device_id={axis: lax.rem(me + j, n)})
            return carry
        lax.fori_loop(1, n, one, 0)

    greet("section", s, n_sec)
    greet("col", k, n_col)
    for to in (y_up, y_down, z_other):
        pl.semaphore_signal(barrier, inc=1, device_id={"row": to})
    pl.semaphore_wait(barrier, n_sec + n_col + 1)

    def sec_issue(c):
        def from_ref(ref, first):
            cols = pl.ds(pl.multiple_of((c - first) * wide, wide), wide)

            def one(j, carry):
                to = lax.rem(s + j, n_sec)
                pltpu.make_async_remote_copy(
                    src_ref=ref.at[0, to, :, cols], dst_ref=piece(c, s),
                    send_sem=sec_send.at[c], recv_sem=sec_recv.at[c], device_id={"section": to},
                ).start()
                return carry
            lax.fori_loop(1, n_sec, one, 0)
            pltpu.make_async_copy(ref.at[0, s, :, cols], piece(c, s), sec_recv.at[c]).start()

        @pl.when(c < half)
        def _():
            from_ref(gate_ref, 0)

        @pl.when(c >= half)
        def _():
            from_ref(up_ref, half)

    def sec_wait(c):
        pltpu.make_async_remote_copy(
            src_ref=block(c, r), dst_ref=block(c, r), send_sem=sec_send.at[c],
            recv_sem=sec_recv.at[c], device_id={"section": lax.rem(s + 1, n_sec)},
        ).wait_recv()

    for c in range(LEAD):
        sec_issue(c)

    def tok_at(which):
        return toks.at[pl.ds(pl.multiple_of(which * n_tok, n_tok), n_tok), :]

    def tok_one(j, carry):
        pltpu.make_async_remote_copy(
            src_ref=tok_ref, dst_ref=tok_at(k), send_sem=tok_send, recv_sem=tok_recv,
            device_id={"col": lax.rem(k + j, n_col)},
        ).start()
        return carry
    lax.fori_loop(1, n_col, tok_one, 0)
    pltpu.make_async_copy(tok_ref, tok_at(k), tok_recv).start()

    def lhs_at(group):
        return lhs.at[:, pl.ds(pl.multiple_of(group * cap, cap), cap)]

    def pick():
        pltpu.make_async_remote_copy(
            src_ref=toks, dst_ref=toks, send_sem=tok_send, recv_sem=tok_recv,
            device_id={"col": lax.rem(k + 1, n_col)},
        ).wait_recv()
        turned = toks[...].T

        def one(e, carry):
            ids = lax.broadcasted_iota(jnp.int32, (toks.shape[0], cap), 0)
            chosen = (ids == slot_ref[0, pl.ds(e, 1), :]).astype(jnp.bfloat16)
            picked[e] = jnp.dot(turned, chosen, preferred_element_type=jnp.float32).astype(jnp.bfloat16)
            return carry
        lax.fori_loop(0, n_sec, one, 0)

    def pick_issue():
        def one(j, carry):
            to = lax.rem(s + j, n_sec)
            pltpu.make_async_remote_copy(
                src_ref=picked.at[to], dst_ref=lhs_at(s), send_sem=pick_send, recv_sem=pick_recv,
                device_id={"section": to},
            ).start()
            return carry
        lax.fori_loop(1, n_sec, one, 0)
        lhs[:, pl.ds(pl.multiple_of(s * cap, cap), cap)] = picked[s]

    def pick_wait():
        most = lhs.at[:, pl.ds(0, (n_sec - 1) * cap)]
        pltpu.make_async_remote_copy(
            src_ref=most, dst_ref=most, send_sem=pick_send, recv_sem=pick_recv,
            device_id={"section": lax.rem(s + 1, n_sec)},
        ).wait_recv()

    def own(c):
        sec_wait(c)
        row_copy(c, r, z_other).start()
        row_copy(c, r, y_up).start()
        row_copy(c, r, y_down).start()

    def first(c):
        across = y_first(c)

        @pl.when(across)
        def _():
            arrived(c, y_down)
            row_copy(c, y_down, z_other).start()

            @pl.when(lax.rem(c, 5) == 0)
            def _():
                row_copy(c, y_down, y_up).start()
            arrived(c, y_up)
            row_copy(c, y_up, z_other).start()

            @pl.when(lax.rem(c, 5) != 0)
            def _():
                row_copy(c, y_up, y_down).start()

        @pl.when(jnp.logical_not(across))
        def _():
            arrived(c, z_other)
            row_copy(c, z_other, y_up).start()
            row_copy(c, z_other, y_down).start()
            arrived(c, y_down)
            row_copy(c, y_down, y_up).start()

    far, far_other = row_at(y + 2, z), row_at(y + 2, 1 - z)
    up_other, down_other = row_at(y + 1, 1 - z), row_at(y - 1, 1 - z)

    def second(c):
        across = y_first(c)

        @pl.when(across)
        def _():
            arrived(c, far)
            row_copy(c, far, z_other).start()

        @pl.when(jnp.logical_not(across))
        def _():
            arrived(c, up_other)
            row_copy(c, up_other, y_down).start()

    def finish(c):
        across = y_first(c)

        @pl.when(across)
        def _():
            arrived(c, z_other)
            arrived(c, up_other)

        @pl.when(jnp.logical_not(across))
        def _():
            arrived(c, y_up)
            arrived(c, far)
        arrived(c, down_other)
        arrived(c, far_other)
        summed = jnp.dot(
            lhs[...], grads[c].reshape(lhs.shape[1], wide), preferred_element_type=jnp.float32
        ).astype(jnp.bfloat16)

        @pl.when(c < half)
        def _():
            out_gate[0, :, pl.ds(pl.multiple_of(c * wide, wide), wide)] = summed

        @pl.when(c >= half)
        def _():
            out_up[0, :, pl.ds(pl.multiple_of((c - half) * wide, wide), wide)] = summed

    def step(t, carry):
        @pl.when(t + LEAD < NC)
        def _():
            sec_issue(t + LEAD)

        @pl.when(t < NC)
        def _():
            own(t)

        @pl.when((t >= 1) & (t < NC + 1))
        def _():
            first(t - 1)

        @pl.when((t >= 2) & (t < NC + 2))
        def _():
            second(t - 2)

        @pl.when(t == 1)
        def _():
            pick()

        @pl.when(t == 2)
        def _():
            pick_issue()

        @pl.when(t == 3)
        def _():
            pick_wait()

        @pl.when(t >= 3)
        def _():
            finish(t - 3)
        return carry
    lax.fori_loop(0, NC + 3, step, 0)

    def sent(ref, sem):
        pltpu.make_async_remote_copy(
            src_ref=ref, dst_ref=ref, send_sem=sem, recv_sem=row_recv.at[0, 0], device_id={"row": y_up},
        ).wait_send()

    sent(toks.at[pl.ds(0, (n_col - 1) * n_tok), :], tok_send)
    sent(lhs.at[:, pl.ds(0, (n_sec - 1) * cap)], pick_send)

    def drain(c, carry):
        sent(grads.at[c, pl.ds(0, n_sec - 1), pl.ds(0, rows), :], sec_send.at[c])
        sent(grads.at[c, :, pl.ds(0, 7 * rows), :], row_send.at[c])
        return carry
    lax.fori_loop(0, NC, drain, 0)


def body(n_sec, n_col, tokens, grad_gate, grad_up, slot_token):
    n_tok, d = tokens.shape
    _, e, rows, f = grad_gate.shape
    cap = slot_token.shape[2]
    wide = 2 * f // NC
    n_row = cap // rows
    dma = pltpu.SemaphoreType.DMA
    any_space = pl.BlockSpec(memory_space=pl.ANY)
    vmem = pl.BlockSpec(memory_space=pltpu.VMEM)
    return pl.pallas_call(
        functools.partial(kernel, n_sec, n_col),
        out_shape=(
            pltpu.VMEM((1, d, f), jnp.bfloat16),
            pltpu.VMEM((1, d, f), jnp.bfloat16),
        ),
        in_specs=[any_space, any_space, any_space, vmem],
        out_specs=(vmem, vmem),
        scratch_shapes=[
            pltpu.VMEM((NC, n_sec, cap, wide), jnp.bfloat16),
            pltpu.VMEM((n_tok * n_col, d), jnp.bfloat16),
            pltpu.VMEM((e, d, cap), jnp.bfloat16),
            pltpu.VMEM((d, n_sec * cap), jnp.bfloat16),
            dma(()), dma(()), dma(()), dma(()),
            dma((NC,)), dma((NC,)), dma((NC,)), dma((NC, n_row)),
        ],
        compiler_params=pltpu.CompilerParams(
            collective_id=0, has_side_effects=True, vmem_limit_bytes=50 * 2**20
        ),
        cost_estimate=pl.CostEstimate(
            flops=4 * n_sec * cap * d * f, bytes_accessed=4 * d * f, transcendentals=0
        ),
    )(tokens, grad_gate, grad_up, slot_token)


def solution(mesh):
    return jax.shard_map(
        functools.partial(body, mesh.shape["section"], mesh.shape["col"]),
        mesh=mesh,
        in_specs=(
            P(("section", "col"), "row"),
            P("section", None, "row", "col"),
            P("section", None, "row", "col"),
            P("section", None, None),
        ),
        out_specs=(P("section", "row", "col"), P("section", "row", "col")),
        check_vma=False,
    )
```

time: 356 us -> 127 us (0.36)
  waiting for transfers between devices: 240 us -> 0 us
  Pallas kernels: 0 us -> 123 us
  blocking collectives: 81.1 us -> 0 us
  matrix products: 14.9 us -> 0 us
  between operations: 14.1 us -> 0.64 us
    all_gather x2 -> x0, waiting for transfers between devices: 240 us -> none  [the longest x1 147 us: body(): lax.all_gather(moved_gate, 'row', axis=2, tiled=True)]
    pallas_call x0 -> x1, Pallas kernels: none -> 123 us  [body(): pl.pallas_call(functools.partial(kernel, n_sec, n_col), out_shape=(pltpu....]
    all_to_all x3 -> x0, blocking collectives: 59.7 us -> none  [the longest x1 21.1 us: body(): lax.all_to_all(grad_up, 'section', split_axis=1, concat_axis=0, tiled=True)]
    all_gather x1 -> x0, blocking collectives: 21.4 us -> none  [body(): group_tokens = lax.all_gather(tokens, 'col', axis=0, tiled=True)]
    dot_general x2 -> x0, matrix products: 14.9 us -> none  [outer_sum(): jnp.einsum('gecd,gecf->edf', picked, grads, preferred_element_type=jnp.fl...]
    gather x1 -> x0, local copies, waits for them, and re-layouts: 3.96 us -> none  [body(): routed = jnp.take(group_tokens, slot_token[0], axis=0)[None]]
    unnamed x2, local copies, waits for them, and re-layouts: 0.01 us -> 3.67 us
  transfers between devices with their start and end apart: 2 -> 0, of which waited for: 2 -> 0; matrix products, arithmetic and copies ran while one was open for 4% -> 0% of each run, Pallas kernels for 0% -> 0%
where the time goes in v1:
time: 127 us
  Pallas kernels  123 us (97%)
  local copies, waits for them, and re-layouts  3.67 us (3%)
    pallas_call x1, Pallas kernels, body(): pl.pallas_call(functools.partial(kernel, n_sec, n_col), out_shape=(pltpu....  123 us
    unnamed x2, local copies, waits for them, and re-layouts  3.67 us

profile of v1, /device:TPU:1, one launch (start us, length us, event | category | flops | bytes accessed | tf_op | source)
XLA Modules:
  0.0 127.4 jit_solution(14645856839384118158)
XLA Ops:
  0.6 123.1 %shard_map.59 = (bf16[1,512,3584]{2,1,0:T(8,128)(2,1)S(1)}, bf16[1,512,3584]{2,1,0:T(8,128)(2,1)S(1)}) custom-call(bf16[128,512]{1,0:T(8,128)(2,1)} %tok_ref.1, bf16[1,8,16,3584]{3,2,1,0:T(8,128)(2,1)} %gate_ref.1, bf16[1,8,16,3584]{3,2,1,0:T(8,128)(2,1)} %up_ref.1, s32[1,8,128]{2,1,0:T(8,128)} %slot_ref.1), custom_call_target="tpu_custom_call" | custom-call | flops 7516192768 | bytes 7340032 | tf_op jit(solution)/shard_map/pallas_call | solution.py:278
  123.7 1.8 %copy.8 = bf16[1,512,3584]{2,1,0:T(8,128)(2,1)} copy(bf16[1,512,3584]{2,1,0:T(8,128)(2,1)S(1)} %get-tuple-element.2) | data formatting | bytes 7340032
  125.5 1.8 %copy.9 = bf16[1,512,3584]{2,1,0:T(8,128)(2,1)} copy(bf16[1,512,3584]{2,1,0:T(8,128)(2,1)S(1)} %get-tuple-element.3) | data formatting | bytes 7340032

commit v2 on v1

v2 whole, which is shorter than its diff:
```python
import functools

import jax
import jax.numpy as jnp
from jax import lax
from jax.experimental import pallas as pl
from jax.experimental.pallas import tpu as pltpu
from jax.sharding import PartitionSpec as P

NC = 14
PAIRS = 4
LEAD = 4
LAG1, LAG2, LAG3 = 4, 5, 6
OTHER0, OWN0 = 8, 10


def pair_start(q):
    return 2 * q + jnp.maximum(q - 1, 0)


def paired(c):
    return (c < 4) | ((c >= 5) & (c < 10) & (lax.rem(c - 5, 3) != 2))


def plane(c):
    return jnp.where(c < 4, lax.rem(c, 2), lax.rem(c - 5, 3))


def kernel(
    n_sec, n_col,
    tok_ref, gate_ref, up_ref, slot_ref, out_gate, out_up,
    grads, toks, chosen, picked, lhs, stage,
    tok_send, tok_recv, pick_send, pick_recv, sec_send, sec_recv, row_send, row_recv, out_send, out_recv,
):
    s, r, k = lax.axis_index("section"), lax.axis_index("row"), lax.axis_index("col")
    y, z = r // 2, lax.rem(r, 2)

    def row_at(yy, zz):
        return lax.rem(yy + 8, 4) * 2 + zz

    y_up, y_down, z_other = row_at(y + 1, z), row_at(y - 1, z), row_at(y, 1 - z)
    far, far_other = row_at(y + 2, z), row_at(y + 2, 1 - z)
    up_other, down_other = row_at(y + 1, 1 - z), row_at(y - 1, 1 - z)
    rows = gate_ref.shape[2]
    wide = grads.shape[3]
    deep = out_gate.shape[1]
    half = NC // 2
    n_tok = tok_ref.shape[0]
    cap = slot_ref.shape[2]

    n_ring = 2 * n_col
    here = k * 2 + z

    def ring_device(w):
        w = lax.rem(w + n_ring, n_ring)
        return {"row": y * 2 + lax.rem(w, 2), "col": w // 2}

    def block(c, who):
        return grads.at[c, :, pl.ds(pl.multiple_of(who * rows, rows), rows), :]

    def piece(c, group):
        return grads.at[c, group, pl.ds(pl.multiple_of(r * rows, rows), rows), :]

    def row_copy(c, who, to):
        return pltpu.make_async_remote_copy(
            src_ref=block(c, who), dst_ref=block(c, who),
            send_sem=row_send.at[c], recv_sem=row_recv.at[c, who], device_id={"row": to},
        )

    def arrived(c, who):
        row_copy(c, who, y_up).wait_recv()

    barrier = pltpu.get_barrier_semaphore()

    def greet(j, carry):
        pl.semaphore_signal(barrier, inc=1, device_id={"section": lax.rem(s + j, n_sec)})
        return carry
    lax.fori_loop(1, n_sec, greet, 0)
    for to in (y_up, y_down):
        pl.semaphore_signal(barrier, inc=1, device_id={"row": to})
    for w in (here + 1, here - 1):
        pl.semaphore_signal(barrier, inc=1, device_id=ring_device(w))

    for e in range(n_sec):
        ids = lax.broadcasted_iota(jnp.int32, (toks.shape[1], cap), 0)
        chosen[:, e * cap : (e + 1) * cap] = (ids == slot_ref[0, e : e + 1, :]).astype(jnp.bfloat16)

    pl.semaphore_wait(barrier, n_sec + 3)

    def tok_at(w):
        w = lax.rem(w + n_ring, n_ring)
        return toks.at[lax.rem(w, 2), pl.ds(pl.multiple_of(w // 2 * n_tok, n_tok), n_tok), :]

    def tok_copy(w, way, src=None):
        return pltpu.make_async_remote_copy(
            src_ref=tok_at(w) if src is None else src, dst_ref=tok_at(w),
            send_sem=tok_send.at[way], recv_sem=tok_recv.at[lax.rem(w + n_ring, n_ring)],
            device_id=ring_device(here + 1 - 2 * way),
        )

    def tok_wait(w):
        tok_copy(w, 0).wait_recv()

    def tok_pass(h):
        tok_wait(here - h)

        @pl.when(h < n_ring // 2)
        def _():
            tok_copy(here - h, 0).start()

        @pl.when(h < n_ring // 2)
        def _():
            tok_wait(here + h)

        @pl.when(h < n_ring // 2 - 1)
        def _():
            tok_copy(here + h, 1).start()

    tok_copy(here, 0, tok_ref).start()
    tok_copy(here, 1, tok_ref).start()
    tok_own = pltpu.make_async_copy(tok_ref, tok_at(here), tok_recv.at[here])
    tok_own.start()

    def sec_issue(c):
        def from_ref(ref, first_chunk):
            cols = pl.ds(pl.multiple_of((c - first_chunk) * wide, wide), wide)

            def one(j, carry):
                to = lax.rem(s + j, n_sec)
                pltpu.make_async_remote_copy(
                    src_ref=ref.at[0, to, :, cols], dst_ref=piece(c, s),
                    send_sem=sec_send.at[c], recv_sem=sec_recv.at[c], device_id={"section": to},
                ).start()
                return carry
            lax.fori_loop(1, n_sec, one, 0)
            pltpu.make_async_copy(ref.at[0, s, :, cols], piece(c, s), sec_recv.at[c]).start()

        @pl.when(c < half)
        def _():
            from_ref(gate_ref, 0)

        @pl.when(c >= half)
        def _():
            from_ref(up_ref, half)

    def sec_wait(c):
        pltpu.make_async_remote_copy(
            src_ref=block(c, r), dst_ref=block(c, r), send_sem=sec_send.at[c],
            recv_sem=sec_recv.at[c], device_id={"section": lax.rem(s + 1, n_sec)},
        ).wait_recv()

    for c in range(LEAD):
        sec_issue(c)

    def features(which):
        return lax.rem(z + 1 + which, 2)

    def lhs_at(which, group):
        return lhs.at[which, :, pl.ds(pl.multiple_of(group * cap, cap), cap)]

    def pick(which):
        found = jnp.dot(
            toks[features(which)].T, chosen[...], preferred_element_type=jnp.float32
        ).astype(jnp.bfloat16)
        for e in range(n_sec):
            picked[which, e] = found[:, e * cap : (e + 1) * cap]

    def pick_issue(which):
        def one(j, carry):
            to = lax.rem(s + j, n_sec)
            pltpu.make_async_remote_copy(
                src_ref=picked.at[which, to], dst_ref=lhs_at(which, s), send_sem=pick_send.at[which],
                recv_sem=pick_recv.at[which], device_id={"section": to},
            ).start()
            return carry
        lax.fori_loop(1, n_sec, one, 0)
        lhs[which, :, pl.ds(pl.multiple_of(s * cap, cap), cap)] = picked[which, s]

    def pick_wait(which):
        most = lhs.at[which, :, pl.ds(0, (n_sec - 1) * cap)]
        pltpu.make_async_remote_copy(
            src_ref=most, dst_ref=most, send_sem=pick_send.at[which], recv_sem=pick_recv.at[which],
            device_id={"section": lax.rem(s + 1, n_sec)},
        ).wait_recv()

    def active(c):
        return jnp.logical_not(paired(c)) | (plane(c) == z)

    def own(c):
        sec_wait(c)

        @pl.when(jnp.logical_not(paired(c)) | (plane(c) != z))
        def _():
            row_copy(c, r, z_other).start()

        @pl.when(active(c))
        def _():
            row_copy(c, r, y_up).start()
            row_copy(c, r, y_down).start()

    def first(c):
        @pl.when(active(c))
        def _():
            arrived(c, z_other)
            row_copy(c, z_other, y_up).start()
            row_copy(c, z_other, y_down).start()
            arrived(c, y_down)
            row_copy(c, y_down, y_up).start()

    def second(c):
        @pl.when(active(c))
        def _():
            arrived(c, up_other)
            row_copy(c, up_other, y_down).start()

    def rest(c):
        for who in (y_up, far, down_other, far_other):
            arrived(c, who)

    def product(which, c):
        return jnp.dot(
            lhs[which], grads[c].reshape(lhs.shape[2], wide), preferred_element_type=jnp.float32
        ).astype(jnp.bfloat16)

    def columns(c, do):
        @pl.when(c < half)
        def _():
            do(out_gate, pl.ds(pl.multiple_of(c * wide, wide), wide))

        @pl.when(c >= half)
        def _():
            do(out_up, pl.ds(pl.multiple_of((c - half) * wide, wide), wide))

    def product_own(c):
        summed = product(1, c)

        def put(ref, cols):
            ref[0, :, cols] = summed
        columns(c, put)

    def out_issue(q, part):
        part_rows = pl.ds(part * (deep // 2), deep // 2)

        def send(ref, cols):
            pltpu.make_async_remote_copy(
                src_ref=stage.at[q, part_rows, :], dst_ref=ref.at[0, part_rows, cols],
                send_sem=out_send.at[q], recv_sem=out_recv.at[q], device_id={"row": z_other},
            ).start()
        columns(pair_start(q) + z, send)

    def out_copy(q):
        return pltpu.make_async_remote_copy(
            src_ref=stage.at[q], dst_ref=stage.at[q], send_sem=out_send.at[q], recv_sem=out_recv.at[q],
            device_id={"row": z_other},
        )

    def other_step(q):
        return jnp.maximum(pair_start(q) + LAG2 + 1, OTHER0)

    def own_step(q):
        return jnp.maximum(pair_start(q) + LAG2 + 3, OWN0 + q)

    def step(t, carry):
        @pl.when(t + LEAD < NC)
        def _():
            sec_issue(t + LEAD)

        @pl.when(t < NC)
        def _():
            own(t)

        @pl.when(t == 0)
        def _():
            tok_pass(1)

        @pl.when(t == 3)
        def _():
            tok_pass(2)

        @pl.when(t == 5)
        def _():
            if n_ring // 2 > 2:
                tok_pass(3)
            pick(0)
            pick_issue(0)

        @pl.when(t == 6)
        def _():
            if n_ring // 2 > 3:
                tok_pass(4)
            tok_own.wait()
            pick(1)

        @pl.when(t == 7)
        def _():
            pick_issue(1)

        @pl.when((t >= LAG1) & (t < NC + LAG1))
        def _():
            first(t - LAG1)

        @pl.when((t >= LAG2) & (t < NC + LAG2))
        def _():
            second(t - LAG2)

        def pair(q, carry):
            for part in range(2):
                @pl.when(t == other_step(q) + 1 + part)
                def _():
                    out_issue(q, part)

            @pl.when(t == other_step(q))
            def _():
                @pl.when(q == 0)
                def _():
                    pick_wait(0)
                rest(pair_start(q) + z)
                stage[q] = product(0, pair_start(q) + z)

            @pl.when(t == own_step(q))
            def _():
                product_own(pair_start(q) + z)
            return carry

        @pl.when(t == OWN0)
        def _():
            pick_wait(1)
        lax.fori_loop(0, PAIRS, pair, 0)

        plain = t - LAG3

        @pl.when((t >= OWN0) & jnp.logical_not(paired(plain)))
        def _():
            rest(plain)
            product_own(plain)
        return carry
    lax.fori_loop(0, NC + LAG3, step, 0)

    def sent(ref, sem):
        pltpu.make_async_remote_copy(
            src_ref=ref, dst_ref=ref, send_sem=sem, recv_sem=row_recv.at[0, 0], device_id={"row": y_up},
        ).wait_send()

    def drain_out(q, carry):
        out_copy(q).wait_recv()
        out_copy(q).wait_send()
        return carry
    lax.fori_loop(0, PAIRS, drain_out, 0)

    sent(toks.at[0], tok_send.at[0])
    sent(toks.at[0, pl.ds(0, (n_col - 1) * n_tok), :], tok_send.at[1])
    for which in range(2):
        sent(lhs.at[which, :, pl.ds(0, (n_sec - 1) * cap)], pick_send.at[which])

    def drain(c, carry):
        sent(grads.at[c, pl.ds(0, n_sec - 1), pl.ds(0, rows), :], sec_send.at[c])

        @pl.when(jnp.logical_not(paired(c)))
        def _():
            sent(grads.at[c, :, pl.ds(0, 7 * rows), :], row_send.at[c])

        @pl.when(paired(c) & active(c))
        def _():
            sent(grads.at[c, :, pl.ds(0, 6 * rows), :], row_send.at[c])

        @pl.when(jnp.logical_not(active(c)))
        def _():
            sent(grads.at[c, :, pl.ds(0, rows), :], row_send.at[c])
        return carry
    lax.fori_loop(0, NC, drain, 0)


def body(n_sec, n_col, tokens, grad_gate, grad_up, slot_token):
    n_tok, d = tokens.shape
    _, e, rows, f = grad_gate.shape
    cap = slot_token.shape[2]
    wide = 2 * f // NC
    n_row = cap // rows
    dma = pltpu.SemaphoreType.DMA
    any_space = pl.BlockSpec(memory_space=pl.ANY)
    vmem = pl.BlockSpec(memory_space=pltpu.VMEM)
    return pl.pallas_call(
        functools.partial(kernel, n_sec, n_col),
        out_shape=(
            pltpu.VMEM((1, d, f), jnp.bfloat16),
            pltpu.VMEM((1, d, f), jnp.bfloat16),
        ),
        in_specs=[any_space, any_space, any_space, vmem],
        out_specs=(vmem, vmem),
        scratch_shapes=[
            pltpu.VMEM((NC, n_sec, cap, wide), jnp.bfloat16),
            pltpu.VMEM((2, n_tok * n_col, d), jnp.bfloat16),
            pltpu.VMEM((n_tok * n_col, n_sec * cap), jnp.bfloat16),
            pltpu.VMEM((2, e, d, cap), jnp.bfloat16),
            pltpu.VMEM((2, d, n_sec * cap), jnp.bfloat16),
            pltpu.VMEM((PAIRS, d, wide), jnp.bfloat16),
            dma((2,)), dma((2 * n_col,)), dma((2,)), dma((2,)),
            dma((NC,)), dma((NC,)), dma((NC,)), dma((NC, n_row)), dma((PAIRS,)), dma((PAIRS,)),
        ],
        compiler_params=pltpu.CompilerParams(
            collective_id=0, has_side_effects=True, vmem_limit_bytes=50 * 2**20
        ),
        cost_estimate=pl.CostEstimate(
            flops=4 * n_sec * cap * d * f, bytes_accessed=4 * d * f, transcendentals=0
        ),
    )(tokens, grad_gate, grad_up, slot_token)


def solution(mesh):
    return jax.shard_map(
        functools.partial(body, mesh.shape["section"], mesh.shape["col"]),
        mesh=mesh,
        in_specs=(
            P(("section", "col"), "row"),
            P("section", None, "row", "col"),
            P("section", None, "row", "col"),
            P("section", None, None),
        ),
        out_specs=(P("section", "row", "col"), P("section", "row", "col")),
        check_vma=False,
    )
```

time: 127 us -> 115 us (0.906)
  the two profiles are of different devices: /device:TPU:1 before, /device:TPU:32 now
where the time goes in v2:
time: 115 us
  Pallas kernels  111 us (97%)
  local copies, waits for them, and re-layouts  3.67 us (3%)
    pallas_call x1, Pallas kernels, body(): pl.pallas_call(functools.partial(kernel, n_sec, n_col), out_shape=(pltpu....  111 us
    unnamed x2, local copies, waits for them, and re-layouts  3.67 us

profile of v2, /device:TPU:32, one launch (start us, length us, event | category | flops | bytes accessed | tf_op | source)
XLA Modules:
  0.0 115.1 jit_solution(2327792229236608674)
XLA Ops:
  0.6 110.8 %shard_map.59 = (bf16[1,512,3584]{2,1,0:T(8,128)(2,1)S(1)}, bf16[1,512,3584]{2,1,0:T(8,128)(2,1)S(1)}) custom-call(bf16[128,512]{1,0:T(8,128)(2,1)} %tok_ref.1, bf16[1,8,16,3584]{3,2,1,0:T(8,128)(2,1)} %gate_ref.1, bf16[1,8,16,3584]{3,2,1,0:T(8,128)(2,1)} %up_ref.1, s32[1,8,128]{2,1,0:T(8,128)} %slot_ref.1), custom_call_target="tpu_custom_call" | custom-call | flops 7516192768 | bytes 7340032 | tf_op jit(solution)/shard_map/pallas_call | solution.py:382
  111.4 1.8 %copy.8 = bf16[1,512,3584]{2,1,0:T(8,128)(2,1)} copy(bf16[1,512,3584]{2,1,0:T(8,128)(2,1)S(1)} %get-tuple-element.2) | data formatting | bytes 7340032
  113.2 1.8 %copy.9 = bf16[1,512,3584]{2,1,0:T(8,128)(2,1)} copy(bf16[1,512,3584]{2,1,0:T(8,128)(2,1)S(1)} %get-tuple-element.3) | data formatting | bytes 7340032

commit v3 on v2

--- a/solution.py
+++ b/solution.py
@@ -8,22 +8,26 @@
 from jax.sharding import PartitionSpec as P
 
 NC = 14
+LOOP = NC - 1
 PAIRS = 4
-LEAD = 4
-LAG1, LAG2, LAG3 = 4, 5, 6
-OTHER0, OWN0 = 8, 10
+BEGIN = 6
+AHEAD = 3
+LEAD = 6
+BEHIND = 11
+LAGZ, LAG1, LAG2, LAG3 = 2, 4, 5, 6
+OTHER0, OWN0 = 7, 10
 
 
 def pair_start(q):
-    return 2 * q + jnp.maximum(q - 1, 0)
+    return 2 * q
 
 
 def paired(c):
-    return (c < 4) | ((c >= 5) & (c < 10) & (lax.rem(c - 5, 3) != 2))
+    return c < 2 * PAIRS
 
 
 def plane(c):
-    return jnp.where(c < 4, lax.rem(c, 2), lax.rem(c - 5, 3))
+    return lax.rem(lax.rem(c, 2) + c // 2, 2)
 
 
 def kernel(
@@ -148,6 +152,15 @@
             src_ref=block(c, r), dst_ref=block(c, r), send_sem=sec_send.at[c],
             recv_sem=sec_recv.at[c], device_id={"section": lax.rem(s + 1, n_sec)},
         ).wait_recv()
+
+    open_cols = pl.ds((half - 1) * wide, wide)
+    open_own = pltpu.make_async_copy(up_ref.at[0, :, :, open_cols], block(NC, r), row_recv.at[NC, r])
+    open_own.start()
+    for to in (y_up, y_down, z_other):
+        pltpu.make_async_remote_copy(
+            src_ref=up_ref.at[0, :, :, open_cols], dst_ref=block(NC, r),
+            send_sem=row_send.at[NC], recv_sem=row_recv.at[NC, r], device_id={"row": to},
+        ).start()
 
     for c in range(LEAD):
         sec_issue(c)
@@ -186,36 +199,69 @@
     def active(c):
         return jnp.logical_not(paired(c)) | (plane(c) == z)
 
-    def own(c):
-        sec_wait(c)
-
+    def own_z(c):
         @pl.when(jnp.logical_not(paired(c)) | (plane(c) != z))
         def _():
             row_copy(c, r, z_other).start()
 
+    def own_y(c):
         @pl.when(active(c))
         def _():
             row_copy(c, r, y_up).start()
             row_copy(c, r, y_down).start()
 
-    def first(c):
+    def other_y(c):
+        arrived(c, z_other)
+        row_copy(c, z_other, y_up).start()
+        row_copy(c, z_other, y_down).start()
+
+    def pass_up(c):
+        arrived(c, y_down)
+        row_copy(c, y_down, y_up).start()
+
+    def pass_down(c):
+        arrived(c, up_other)
+        row_copy(c, up_other, y_down).start()
+
+    def if_active(c, do):
         @pl.when(active(c))
         def _():
-            arrived(c, z_other)
-            row_copy(c, z_other, y_up).start()
-            row_copy(c, z_other, y_down).start()
-            arrived(c, y_down)
-            row_copy(c, y_down, y_up).start()
-
-    def second(c):
-        @pl.when(active(c))
-        def _():
-            arrived(c, up_other)
-            row_copy(c, up_other, y_down).start()
+            do(c)
+
+    def pass_both(c):
+        pass_up(c)
+        pass_down(c)
 
     def rest(c):
         for who in (y_up, far, down_other, far_other):
             arrived(c, who)
+
+    def open_copy(to):
+        return pltpu.make_async_remote_copy(
+            src_ref=grads.at[NC, to], dst_ref=grads.at[LOOP, s],
+            send_sem=sec_send.at[LOOP], recv_sem=sec_recv.at[LOOP], device_id={"section": to},
+        )
+
+    def open_exchange():
+        open_own.wait()
+        rest(NC)
+
+        def one(j, carry):
+            open_copy(lax.rem(s + j, n_sec)).start()
+            return carry
+        lax.fori_loop(1, n_sec, one, 0)
+        grads[LOOP, s] = grads[NC, s]
+
+    def open_most():
+        most = grads.at[LOOP, pl.ds(0, n_sec - 1)]
+        return pltpu.make_async_remote_copy(
+            src_ref=most, dst_ref=most, send_sem=sec_send.at[LOOP], recv_sem=sec_recv.at[LOOP],
+            device_id={"section": lax.rem(s + 1, n_sec)},
+        )
+
+    def open_finish():
+        open_most().wait_recv()
+        product_own(LOOP)
 
     def product(which, c):
         return jnp.dot(
@@ -238,15 +284,13 @@
             ref[0, :, cols] = summed
         columns(c, put)
 
-    def out_issue(q, part):
-        part_rows = pl.ds(part * (deep // 2), deep // 2)
-
+    def out_issue(q):
         def send(ref, cols):
             pltpu.make_async_remote_copy(
-                src_ref=stage.at[q, part_rows, :], dst_ref=ref.at[0, part_rows, cols],
+                src_ref=stage.at[q], dst_ref=ref.at[0, :, cols],
                 send_sem=out_send.at[q], recv_sem=out_recv.at[q], device_id={"row": z_other},
             ).start()
-        columns(pair_start(q) + z, send)
+        columns(pair_start(q) + lax.rem(z + q, 2), send)
 
     def out_copy(q):
         return pltpu.make_async_remote_copy(
@@ -261,65 +305,54 @@
         return jnp.maximum(pair_start(q) + LAG2 + 3, OWN0 + q)
 
     def step(t, carry):
-        @pl.when(t + LEAD < NC)
-        def _():
-            sec_issue(t + LEAD)
-
-        @pl.when(t < NC)
-        def _():
-            own(t)
-
-        @pl.when(t == 0)
-        def _():
-            tok_pass(1)
-
-        @pl.when(t == 3)
-        def _():
-            tok_pass(2)
-
-        @pl.when(t == 5)
-        def _():
-            if n_ring // 2 > 2:
-                tok_pass(3)
-            pick(0)
-            pick_issue(0)
-
-        @pl.when(t == 6)
-        def _():
-            if n_ring // 2 > 3:
-                tok_pass(4)
-            tok_own.wait()
-            pick(1)
-
-        @pl.when(t == 7)
+        @pl.when(t + AHEAD < LOOP)
+        def _():
+            sec_wait(t + AHEAD)
+            own_z(t + AHEAD)
+
+        def out_step(q, carry):
+            @pl.when(t == other_step(q) + 1)
+            def _():
+                out_issue(q)
+            return carry
+        lax.fori_loop(0, PAIRS, out_step, 0)
+
+        @pl.when(t < LOOP)
+        def _():
+            own_y(t)
+
+        @pl.when(t == BEGIN)
         def _():
             pick_issue(1)
 
-        @pl.when((t >= LAG1) & (t < NC + LAG1))
-        def _():
-            first(t - LAG1)
-
-        @pl.when((t >= LAG2) & (t < NC + LAG2))
-        def _():
-            second(t - LAG2)
+        @pl.when(t < LOOP + LAGZ)
+        def _():
+            if_active(t - LAGZ, other_y)
+
+        @pl.when(t < LOOP + LAG1)
+        def _():
+            if_active(t - LAG1, pass_both)
+
+        @pl.when(t == BEGIN + 1)
+        def _():
+            open_exchange()
+
+        @pl.when(t == LOOP)
+        def _():
+            open_finish()
 
         def pair(q, carry):
-            for part in range(2):
-                @pl.when(t == other_step(q) + 1 + part)
-                def _():
-                    out_issue(q, part)
-
             @pl.when(t == other_step(q))
             def _():
                 @pl.when(q == 0)
                 def _():
                     pick_wait(0)
-                rest(pair_start(q) + z)
-                stage[q] = product(0, pair_start(q) + z)
+                rest(pair_start(q) + lax.rem(z + q, 2))
+                stage[q] = product(0, pair_start(q) + lax.rem(z + q, 2))
 
             @pl.when(t == own_step(q))
             def _():
-                product_own(pair_start(q) + z)
+                product_own(pair_start(q) + lax.rem(z + q, 2))
             return carry
 
         @pl.when(t == OWN0)
@@ -334,7 +367,51 @@
             rest(plain)
             product_own(plain)
         return carry
-    lax.fori_loop(0, NC + LAG3, step, 0)
+
+    tok_pass(1)
+    sec_wait(0)
+    own_z(0)
+    own_y(0)
+    pass_up(NC)
+    sec_wait(1)
+    own_z(1)
+    own_y(1)
+    other_y(NC)
+    sec_issue(LEAD)
+    sec_issue(LEAD + 1)
+    sec_wait(2)
+    own_y(2)
+    tok_pass(2)
+    for c in (3, 4):
+        sec_wait(c)
+        own_y(c)
+    for c in range(LEAD + 2, BEHIND):
+        sec_issue(c)
+    if_active(0, other_y)
+    if_active(1, other_y)
+    pass_down(NC)
+    if n_ring // 2 > 2:
+        tok_pass(3)
+    pick(0)
+    for c in (2, 3, 4):
+        own_z(c)
+    pick_issue(0)
+    for c in range(BEHIND, LOOP):
+        sec_issue(c)
+    for c in range(5, BEGIN + AHEAD):
+        sec_wait(c)
+        own_z(c)
+        if c < BEGIN:
+            own_y(c)
+    if_active(0, pass_both)
+    if_active(1, pass_both)
+    if n_ring // 2 > 3:
+        tok_pass(4)
+    tok_own.wait()
+    pick(1)
+    if_active(2, other_y)
+    if_active(3, other_y)
+    lax.fori_loop(BEGIN, LOOP + LAG3, step, 0)
 
     def sent(ref, sem):
         pltpu.make_async_remote_copy(
@@ -367,7 +444,9 @@
         def _():
             sent(grads.at[c, :, pl.ds(0, rows), :], row_send.at[c])
         return carry
-    lax.fori_loop(0, NC, drain, 0)
+    lax.fori_loop(0, LOOP, drain, 0)
+    open_most().wait_send()
+    sent(grads.at[NC, :, pl.ds(0, 7 * rows), :], row_send.at[NC])
 
 
 def body(n_sec, n_col, tokens, grad_gate, grad_up, slot_token):
@@ -388,14 +467,14 @@
         in_specs=[any_space, any_space, any_space, vmem],
         out_specs=(vmem, vmem),
         scratch_shapes=[
-            pltpu.VMEM((NC, n_sec, cap, wide), jnp.bfloat16),
+            pltpu.VMEM((NC + 1, n_sec, cap, wide), jnp.bfloat16),
             pltpu.VMEM((2, n_tok * n_col, d), jnp.bfloat16),
             pltpu.VMEM((n_tok * n_col, n_sec * cap), jnp.bfloat16),
             pltpu.VMEM((2, e, d, cap), jnp.bfloat16),
             pltpu.VMEM((2, d, n_sec * cap), jnp.bfloat16),
             pltpu.VMEM((PAIRS, d, wide), jnp.bfloat16),
             dma((2,)), dma((2 * n_col,)), dma((2,)), dma((2,)),
-            dma((NC,)), dma((NC,)), dma((NC,)), dma((NC, n_row)), dma((PAIRS,)), dma((PAIRS,)),
+            dma((NC,)), dma((NC,)), dma((NC + 1,)), dma((NC + 1, n_row)), dma((PAIRS,)), dma((PAIRS,)),
         ],
         compiler_params=pltpu.CompilerParams(
             collective_id=0, has_side_effects=True, vmem_limit_bytes=50 * 2**20

time: 115 us -> 106 us (0.922)
  the two profiles are of different devices: /device:TPU:32 before, /device:TPU:1 now
where the time goes in v3:
time: 106 us
  Pallas kernels  101 us (95%)
  local copies, waits for them, and re-layouts  3.67 us (3%)
    pallas_call x1, Pallas kernels, body(): pl.pallas_call(functools.partial(kernel, n_sec, n_col), out_shape=(pltpu....  101 us
    unnamed x2, local copies, waits for them, and re-layouts  3.67 us

profile of v3, /device:TPU:1, one launch (start us, length us, event | category | flops | bytes accessed | tf_op | source)
XLA Modules:
  0.0 105.5 jit_solution(13135543902551069840)
XLA Ops:
  0.6 101.2 %shard_map.59 = (bf16[1,512,3584]{2,1,0:T(8,128)(2,1)S(1)}, bf16[1,512,3584]{2,1,0:T(8,128)(2,1)S(1)}) custom-call(bf16[128,512]{1,0:T(8,128)(2,1)} %tok_ref.1, bf16[1,8,16,3584]{3,2,1,0:T(8,128)(2,1)} %gate_ref.1, bf16[1,8,16,3584]{3,2,1,0:T(8,128)(2,1)} %up_ref.1, s32[1,8,128]{2,1,0:T(8,128)} %slot_ref.1), custom_call_target="tpu_custom_call" | custom-call | flops 7516192768 | bytes 7340032 | tf_op jit(solution)/shard_map/pallas_call | solution.py:461
  101.8 1.8 %copy.8 = bf16[1,512,3584]{2,1,0:T(8,128)(2,1)} copy(bf16[1,512,3584]{2,1,0:T(8,128)(2,1)S(1)} %get-tuple-element.2) | data formatting | bytes 7340032
  103.7 1.8 %copy.9 = bf16[1,512,3584]{2,1,0:T(8,128)(2,1)} copy(bf16[1,512,3584]{2,1,0:T(8,128)(2,1)S(1)} %get-tuple-element.3) | data formatting | bytes 7340032

commit v4 on v3

--- a/solution.py
+++ b/solution.py
@@ -8,7 +8,8 @@
 from jax.sharding import PartitionSpec as P
 
 NC = 14
-LOOP = NC - 1
+OPEN = 2
+LOOP = NC - OPEN
 PAIRS = 4
 BEGIN = 6
 AHEAD = 3
@@ -106,17 +107,21 @@
         tok_copy(w, 0).wait_recv()
 
     def tok_pass(h):
-        tok_wait(here - h)
-
-        @pl.when(h < n_ring // 2)
+        origin = lax.rem(here + h, 2)
+
+        @pl.when(h <= n_col - origin)
+        def _():
+            tok_wait(here - h)
+
+        @pl.when(h < n_col - origin)
         def _():
             tok_copy(here - h, 0).start()
 
-        @pl.when(h < n_ring // 2)
+        @pl.when(h <= n_col - 1 + origin)
         def _():
             tok_wait(here + h)
 
-        @pl.when(h < n_ring // 2 - 1)
+        @pl.when(h < n_col - 1 + origin)
         def _():
             tok_copy(here + h, 1).start()
 
@@ -153,14 +158,23 @@
             recv_sem=sec_recv.at[c], device_id={"section": lax.rem(s + 1, n_sec)},
         ).wait_recv()
 
-    open_cols = pl.ds((half - 1) * wide, wide)
-    open_own = pltpu.make_async_copy(up_ref.at[0, :, :, open_cols], block(NC, r), row_recv.at[NC, r])
-    open_own.start()
-    for to in (y_up, y_down, z_other):
+    def open_src(i):
+        return up_ref.at[0, :, :, pl.ds((half - OPEN + i) * wide, wide)]
+
+    def open_local(i):
+        return pltpu.make_async_copy(open_src(i), block(NC + i, r), row_recv.at[NC + i, r])
+
+    def open_own(i, to):
         pltpu.make_async_remote_copy(
-            src_ref=up_ref.at[0, :, :, open_cols], dst_ref=block(NC, r),
-            send_sem=row_send.at[NC], recv_sem=row_recv.at[NC, r], device_id={"row": to},
+            src_ref=open_src(i), dst_ref=block(NC + i, r),
+            send_sem=row_send.at[NC + i], recv_sem=row_recv.at[NC + i, r], device_id={"row": to},
         ).start()
+
+    for i in range(OPEN):
+        open_local(i).start()
+        open_own(i, y_up)
+        open_own(i, y_down)
+    open_own(0, z_other)
 
     for c in range(LEAD):
         sec_issue(c)
@@ -236,32 +250,30 @@
         for who in (y_up, far, down_other, far_other):
             arrived(c, who)
 
-    def open_copy(to):
-        return pltpu.make_async_remote_copy(
-            src_ref=grads.at[NC, to], dst_ref=grads.at[LOOP, s],
-            send_sem=sec_send.at[LOOP], recv_sem=sec_recv.at[LOOP], device_id={"section": to},
-        )
-
-    def open_exchange():
-        open_own.wait()
-        rest(NC)
+    def open_exchange(i):
+        open_local(i).wait()
+        rest(NC + i)
 
         def one(j, carry):
-            open_copy(lax.rem(s + j, n_sec)).start()
+            to = lax.rem(s + j, n_sec)
+            pltpu.make_async_remote_copy(
+                src_ref=grads.at[NC + i, to], dst_ref=grads.at[LOOP + i, s],
+                send_sem=sec_send.at[LOOP + i], recv_sem=sec_recv.at[LOOP + i], device_id={"section": to},
+            ).start()
             return carry
         lax.fori_loop(1, n_sec, one, 0)
-        grads[LOOP, s] = grads[NC, s]
-
-    def open_most():
-        most = grads.at[LOOP, pl.ds(0, n_sec - 1)]
+        grads[LOOP + i, s] = grads[NC + i, s]
+
+    def open_most(i):
+        most = grads.at[LOOP + i, pl.ds(0, n_sec - 1)]
         return pltpu.make_async_remote_copy(
-            src_ref=most, dst_ref=most, send_sem=sec_send.at[LOOP], recv_sem=sec_recv.at[LOOP],
+            src_ref=most, dst_ref=most, send_sem=sec_send.at[LOOP + i], recv_sem=sec_recv.at[LOOP + i],
             device_id={"section": lax.rem(s + 1, n_sec)},
         )
 
-    def open_finish():
-        open_most().wait_recv()
-        product_own(LOOP)
+    def open_finish(i):
+        open_most(i).wait_recv()
+        product_own(LOOP + i)
 
     def product(which, c):
         return jnp.dot(
@@ -333,13 +345,14 @@
         def _():
             if_active(t - LAG1, pass_both)
 
-        @pl.when(t == BEGIN + 1)
-        def _():
-            open_exchange()
-
-        @pl.when(t == LOOP)
-        def _():
-            open_finish()
+        for i in range(OPEN):
+            @pl.when(t == BEGIN + 1 + i)
+            def _():
+                open_exchange(i)
+
+        @pl.when((t >= LOOP) & (t < NC))
+        def _():
+            open_finish(t - LOOP)
 
         def pair(q, carry):
             @pl.when(t == other_step(q))
@@ -369,6 +382,8 @@
         return carry
 
     tok_pass(1)
+    for i in range(1, OPEN):
+        open_own(i, z_other)
     sec_wait(0)
     own_z(0)
     own_y(0)
@@ -381,12 +396,16 @@
     sec_issue(LEAD + 1)
     sec_wait(2)
     own_y(2)
+    for i in range(1, OPEN):
+        pass_up(NC + i)
     tok_pass(2)
     for c in (3, 4):
         sec_wait(c)
         own_y(c)
     for c in range(LEAD + 2, BEHIND):
         sec_issue(c)
+    for i in range(1, OPEN):
+        other_y(NC + i)
     if_active(0, other_y)
     if_active(1, other_y)
     pass_down(NC)
@@ -403,6 +422,8 @@
         own_z(c)
         if c < BEGIN:
             own_y(c)
+    for i in range(1, OPEN):
+        pass_down(NC + i)
     if_active(0, pass_both)
     if_active(1, pass_both)
     if n_ring // 2 > 3:
@@ -424,8 +445,8 @@
         return carry
     lax.fori_loop(0, PAIRS, drain_out, 0)
 
-    sent(toks.at[0], tok_send.at[0])
-    sent(toks.at[0, pl.ds(0, (n_col - 1) * n_tok), :], tok_send.at[1])
+    sent(toks.at[0, pl.ds(0, (n_col - 1) * n_tok), :], tok_send.at[z])
+    sent(toks.at[0], tok_send.at[1 - z])
     for which in range(2):
         sent(lhs.at[which, :, pl.ds(0, (n_sec - 1) * cap)], pick_send.at[which])
 
@@ -445,8 +466,9 @@
             sent(grads.at[c, :, pl.ds(0, rows), :], row_send.at[c])
         return carry
     lax.fori_loop(0, LOOP, drain, 0)
-    open_most().wait_send()
-    sent(grads.at[NC, :, pl.ds(0, 7 * rows), :], row_send.at[NC])
+    for i in range(OPEN):
+        open_most(i).wait_send()
+        sent(grads.at[NC, :, pl.ds(0, 7 * rows), :], row_send.at[NC + i])
 
 
 def body(n_sec, n_col, tokens, grad_gate, grad_up, slot_token):
@@ -458,7 +480,7 @@
     dma = pltpu.SemaphoreType.DMA
     any_space = pl.BlockSpec(memory_space=pl.ANY)
     vmem = pl.BlockSpec(memory_space=pltpu.VMEM)
-    return pl.pallas_call(
+    gate, up = pl.pallas_call(
         functools.partial(kernel, n_sec, n_col),
         out_shape=(
             pltpu.VMEM((1, d, f), jnp.bfloat16),
@@ -467,14 +489,14 @@
         in_specs=[any_space, any_space, any_space, vmem],
         out_specs=(vmem, vmem),
         scratch_shapes=[
-            pltpu.VMEM((NC + 1, n_sec, cap, wide), jnp.bfloat16),
+            pltpu.VMEM((NC + OPEN, n_sec, cap, wide), jnp.bfloat16),
             pltpu.VMEM((2, n_tok * n_col, d), jnp.bfloat16),
             pltpu.VMEM((n_tok * n_col, n_sec * cap), jnp.bfloat16),
             pltpu.VMEM((2, e, d, cap), jnp.bfloat16),
             pltpu.VMEM((2, d, n_sec * cap), jnp.bfloat16),
             pltpu.VMEM((PAIRS, d, wide), jnp.bfloat16),
             dma((2,)), dma((2 * n_col,)), dma((2,)), dma((2,)),
-            dma((NC,)), dma((NC,)), dma((NC + 1,)), dma((NC + 1, n_row)), dma((PAIRS,)), dma((PAIRS,)),
+            dma((NC,)), dma((NC,)), dma((NC + OPEN,)), dma((NC + OPEN, n_row)), dma((PAIRS,)), dma((PAIRS,)),
         ],
         compiler_params=pltpu.CompilerParams(
             collective_id=0, has_side_effects=True, vmem_limit_bytes=50 * 2**20
@@ -483,6 +505,26 @@
             flops=4 * n_sec * cap * d * f, bytes_accessed=4 * d * f, transcendentals=0
         ),
     )(tokens, grad_gate, grad_up, slot_token)
+    shape = jax.ShapeDtypeStruct((1, d, f), jnp.bfloat16)
+    return pl.pallas_call(
+        settle,
+        out_shape=(shape, shape),
+        in_specs=[vmem, vmem],
+        out_specs=(any_space, any_space),
+        scratch_shapes=[dma((2,))],
+        compiler_params=pltpu.CompilerParams(vmem_limit_bytes=2 * 2**20),
+    )(gate, up)
+
+
+def settle(gate_in, up_in, gate_out, up_out, sems):
+    pieces = 8
+    step = gate_in.shape[1] // pieces
+    for j, (ref, out) in enumerate(((gate_in, gate_out), (up_in, up_out))):
+        for i in range(pieces):
+            rows = pl.ds(i * step, step)
+            pltpu.make_async_copy(ref.at[:, rows, :], out.at[:, rows, :], sems.at[j]).start()
+    pltpu.make_async_copy(gate_in, gate_out, sems.at[0]).wait()
+    pltpu.make_async_copy(up_in, up_out, sems.at[1]).wait()
 
 
 def solution(mesh):

time: 106 us -> 102 us (0.962)
  local copies, waits for them, and re-layouts: 3.67 us -> 0 us
    unnamed x2 -> x0, local copies, waits for them, and re-layouts: 3.67 us -> none
    pallas_call x0 -> x1, Pallas kernels: none -> 2.98 us  [body(): pl.pallas_call(settle, out_shape=(shape, shape), in_specs=[vmem, vmem], o...]
    pallas_call x1, Pallas kernels: 101 us -> 98.5 us  [body(): pl.pallas_call(functools.partial(kernel, n_sec, n_col), out_shape=(pltpu....]
where the time goes in v4:
time: 102 us
  Pallas kernels  101 us (99%)
    pallas_call x1, Pallas kernels, body(): pl.pallas_call(functools.partial(kernel, n_sec, n_col), out_shape=(pltpu....  98.5 us
    pallas_call x1, Pallas kernels, body(): pl.pallas_call(settle, out_shape=(shape, shape), in_specs=[vmem, vmem], o...  2.98 us

profile of v4, /device:TPU:1, one launch (start us, length us, event | category | flops | bytes accessed | tf_op | source)
XLA Modules:
  0.0 102.1 jit_solution(17818225837441853153)
XLA Ops:
  0.6 98.5 %shard_map.59 = (bf16[1,512,3584]{2,1,0:T(8,128)(2,1)S(1)}, bf16[1,512,3584]{2,1,0:T(8,128)(2,1)S(1)}) custom-call(bf16[128,512]{1,0:T(8,128)(2,1)} %tok_ref.1, bf16[1,8,16,3584]{3,2,1,0:T(8,128)(2,1)} %gate_ref.1, bf16[1,8,16,3584]{3,2,1,0:T(8,128)(2,1)} %up_ref.1, s32[1,8,128]{2,1,0:T(8,128)} %slot_ref.1), custom_call_target="tpu_custom_call" | custom-call | flops 7516192768 | bytes 7340032 | tf_op jit(solution)/shard_map/pallas_call | solution.py:483
  99.1 3.0 %shard_map.60 = (bf16[1,512,3584]{2,1,0:T(8,128)(2,1)}, bf16[1,512,3584]{2,1,0:T(8,128)(2,1)}) custom-call(bf16[1,512,3584]{2,1,0:T(8,128)(2,1)S(1)} %get-tuple-element.4.gate_in, bf16[1,512,3584]{2,1,0:T(8,128)(2,1)S(1)} %get-tuple-element.5.up_in), custom_call_target="tpu_custom_call" | custom-call | tf_op jit(solution)/shard_map/pallas_call | solution.py:509

commit v5 on v4

--- a/solution.py
+++ b/solution.py
@@ -15,7 +15,7 @@
 AHEAD = 3
 LEAD = 6
 BEHIND = 11
-LAGZ, LAG1, LAG2, LAG3 = 2, 4, 5, 6
+LAGZ, LAG1, LAG2, LAG3 = 1, 4, 5, 6
 OTHER0, OWN0 = 7, 10
 
 
@@ -432,6 +432,7 @@
     pick(1)
     if_active(2, other_y)
     if_active(3, other_y)
+    if_active(4, other_y)
     lax.fori_loop(BEGIN, LOOP + LAG3, step, 0)
 
     def sent(ref, sem):

time: 102 us -> 102 us (level)
  no operation moved by 1% of the time
where the time goes in v5:
time: 102 us
  Pallas kernels  101 us (99%)
    pallas_call x1, Pallas kernels, body(): pl.pallas_call(functools.partial(kernel, n_sec, n_col), out_shape=(pltpu....  98.5 us
    pallas_call x1, Pallas kernels, body(): pl.pallas_call(settle, out_shape=(shape, shape), in_specs=[vmem, vmem], o...  2.98 us

profile of v5, /device:TPU:1, one launch (start us, length us, event | category | flops | bytes accessed | tf_op | source)
XLA Modules:
  0.0 102.1 jit_solution(14189866477667957929)
XLA Ops:
  0.6 98.5 %shard_map.59 = (bf16[1,512,3584]{2,1,0:T(8,128)(2,1)S(1)}, bf16[1,512,3584]{2,1,0:T(8,128)(2,1)S(1)}) custom-call(bf16[128,512]{1,0:T(8,128)(2,1)} %tok_ref.1, bf16[1,8,16,3584]{3,2,1,0:T(8,128)(2,1)} %gate_ref.1, bf16[1,8,16,3584]{3,2,1,0:T(8,128)(2,1)} %up_ref.1, s32[1,8,128]{2,1,0:T(8,128)} %slot_ref.1), custom_call_target="tpu_custom_call" | custom-call | flops 7516192768 | bytes 7340032 | tf_op jit(solution)/shard_map/pallas_call | solution.py:484
  99.1 3.0 %shard_map.60 = (bf16[1,512,3584]{2,1,0:T(8,128)(2,1)}, bf16[1,512,3584]{2,1,0:T(8,128)(2,1)}) custom-call(bf16[1,512,3584]{2,1,0:T(8,128)(2,1)S(1)} %get-tuple-element.4.gate_in, bf16[1,512,3584]{2,1,0:T(8,128)(2,1)S(1)} %get-tuple-element.5.up_in), custom_call_target="tpu_custom_call" | custom-call | tf_op jit(solution)/shard_map/pallas_call | solution.py:510
